TPU v7x, 32 devices: a whole 2x2x4 slice. The times are simulated.
32 devices in a mesh: grp: 2 (over x), dom: 16 (over z, y, core).
Axes of the slice: x: 2, y: 2, z: 4, core: 2. Of those that a mesh axis runs over, the one named last changes fastest.
Arguments:
- surplus: float32 [48, 64, 4096], P('grp', None, 'dom'), may hold values from -40 to 40
- levels: int32 [48, 3], P('grp'), may hold values from 0 to 3
Outputs:
- updated: float32 [48, 64, 4096], P('grp', None, 'dom')
- coefficients: float32 [48], replicated
All inputs are finite; a program needn't handle non-finite values.
Results may differ from a plain program's by a relative error of at most 0.0003.
Values sent between devices are 32-bit elements; how exact they have to be, the bound alone decides.
A program may use at most 64 MiB of HBM per device.

v0:
```python
import jax
import jax.numpy as jnp
from jax import lax
from jax.sharding import PartitionSpec as P


def owned(levels, count):
    indices = jnp.arange(count, dtype=jnp.int32)
    digits = jnp.stack([indices // 16, indices // 4 % 4, indices % 4])
    return jnp.all(digits[None] <= levels[:, :, None], axis=1).astype(jnp.float32)


def solve_weights(gram_matrix):
    number = gram_matrix.shape[0]
    diagonal_part = jnp.diagonal(gram_matrix) + 1e-06
    scaling = 1.0 / jnp.sqrt(diagonal_part)
    system = scaling[:, None] * gram_matrix * scaling[None, :] + 0.1 * jnp.eye(
        number, dtype=jnp.float32
    )
    factor = jnp.linalg.cholesky(system)
    target = jnp.sqrt(diagonal_part)[:, None]
    halfway = lax.linalg.triangular_solve(factor, target, left_side=True, lower=True)
    weights = lax.linalg.triangular_solve(
        factor, halfway, left_side=True, lower=True, transpose_a=True
    )
    return scaling * weights[:, 0]


def inner_rows(left_rows, right_rows):
    return lax.dot_general(
        left_rows,
        right_rows,
        (((1,), (1,)), ((), ())),
        precision=lax.Precision.HIGHEST,
        preferred_element_type=jnp.float32,
    )


def shards(surplus, levels):
    local_count = surplus.shape[0]
    subspaces = surplus.shape[1]
    grid_total = local_count * lax.axis_size("grp")
    owners = owned(levels, subspaces)
    masked = surplus * owners[:, :, None]
    flattened = masked.reshape(local_count, -1)
    portion = lax.all_gather(masked, "grp", axis=0, tiled=True)
    products = inner_rows(flattened, portion.reshape(portion.shape[0], -1))
    row_start = lax.axis_index("grp") * local_count
    placed = lax.dynamic_update_slice(
        jnp.zeros((grid_total, grid_total), jnp.float32), products, (row_start, jnp.int32(0))
    )
    gram_matrix = lax.psum(placed, ("grp", "dom"))
    coefficients = solve_weights(gram_matrix)
    own_weights = lax.dynamic_slice_in_dim(
        coefficients, lax.axis_index("grp") * local_count, local_count
    )
    partial_sum = jnp.tensordot(own_weights, masked, axes=1, precision=lax.Precision.HIGHEST)
    own_share = lax.psum_scatter(partial_sum, "grp", scatter_dimension=0, tiled=True)
    combined = lax.all_gather(own_share, "grp", axis=0, tiled=True)
    updated = owners[:, :, None] * combined[None]
    return (updated, coefficients)


def solution(mesh):
    placed = (P("grp", None, "dom"), P("grp", None))
    return jax.shard_map(
        shards, mesh=mesh, in_specs=placed, out_specs=(P("grp", None, "dom"), P()), check_vma=False
    )
```

profile of v0, /device:TPU:0, one launch (start us, length us, event | category | flops | bytes accessed | tf_op | source)
XLA Modules:
  0.0 140.4 jit_solution(13781790527731997911)
XLA Ops:
  7.2 0.0 all-gather.2.cloned.1.call-start
  7.3 0.8 compare_reduce_fusion
  8.0 0.1 copy.12
  8.1 3.5 %copy_multiply_fusion = f32[24,64,256]{2,0,1:T(8,128)} fusion(f32[24,64,256]{2,1,0:T(8,128)} %param.2, f32[24,64]{0,1:T(8,128)S(1)} %copy.12), kind=kLoop, calls=%fused_computation.1 | loop fusion | flops 393216 | bytes 3151872 | tf_op jit(solution)/shard_map/mul | solution.py:44
  11.6 0.0 copy-start
  11.6 0.0 all-gather.2.cloned.1.call-update
  11.6 0.0 reduce-scatter.2.cloned.1.call-start
  11.7 47.7 %all-gather.2.cloned.1.call-done = f32[48,64,256]{2,0,1:T(8,128)} async-done(((f32[24,64,256]{2,0,1:T(8,128)}), f32[48,64,256]{2,0,1:T(8,128)}) %all-gather.2.cloned.1.call-update) | async-done | bytes 3145744 | tf_op jit(solution)/shard_map/all_gather | solution.py:46
  59.4 0.0 copy-done
  59.4 4.5 %fusion = f32[48,48]{1,0:T(8,128)S(1)} fusion(f32[48,48]{1,0:T(8,128)S(1)} %broadcast_in_dim.5, s32[]{:T(128)S(6)} %select_n.63, f32[24,64,256]{2,0,1:T(8,128)S(1)} %copy-done, f32[48,64,256]{2,0,1:T(8,128)} %all-gather.2.cloned.1.call-done), kind=kOutput, calls=%fused_computation.3 | convolution fusion | flops 226492416 | bytes 4730884 | tf_op jit(solution)/shard_map/dot_general | solution.py:30
  63.9 39.5 %psum.7 = f32[48,48]{1,0:T(8,128)S(1)} all-reduce(f32[48,48]{1,0:T(8,128)S(1)} %fusion), channel_id=1, replica_groups=mesh['grp'=2,'dom'=16] {'grp','dom'}, use_global_device_ids=true, to_apply=%region_1.2 | all-reduce | flops 2304 | bytes 18432 | tf_op jit(solution)/shard_map/psum | solution.py:52
  103.4 1.0 gather_fusion
  104.4 0.1 select_add_fusion
  104.4 0.1 copy.14
  104.5 0.1 fusion.5
  104.6 4.4 %cholesky.16 = f32[48,48]{1,0:T(8,128)S(1)} custom-call(f32[48,48]{1,0:T(8,128)S(1)} %fusion.5), custom_call_target="Cholesky" | custom-call | tf_op jit(solution)/shard_map/jit(cholesky)/cholesky | solution.py:20
  109.0 0.6 compare_reduce_fusion.1
  109.7 0.7 fusion.2
  110.3 3.7 %custom-call.8 = f32[1,48,48]{1,2,0:T(8,128)S(1)} custom-call(f32[1,48,48]{2,1,0:T(8,128)S(1)} %fusion.2), custom_call_target="InvertDiagBlocksLowerTriangular" | custom-call | tf_op jit(solution)/shard_map/triangular_solve | solution.py:23
  114.0 0.1 convolution_bitcast_fusion.2
  114.1 0.2 fusion.1
  114.3 0.0 copy-start.1
  114.3 1.0 fusion.7
  115.3 0.6 copy.19
  115.9 0.0 reduce-scatter.2.cloned.1.call-update
  116.0 10.9 %reduce-scatter.2.cloned.1.call-done = f32[32,256]{1,0:T(8,128)} async-done(((f32[64,256]{1,0:T(8,128)}), f32[32,256]{1,0:T(8,128)}) %reduce-scatter.2.cloned.1.call-update) | async-done | bytes 32784 | tf_op jit(solution)/shard_map/reduce_scatter | solution.py:58
  126.9 4.8 %all_gather.7 = f32[64,256]{1,0:T(8,128)S(1)} all-gather(f32[32,256]{1,0:T(8,128)} %reduce-scatter.2.cloned.1.call-done), channel_id=1, replica_groups=mesh['grp'=2,'dom'=16] {'grp'}, dimensions={0}, use_global_device_ids=true | all-gather | bytes 98304 | tf_op jit(solution)/shard_map/all_gather | solution.py:59
  131.7 0.3 broadcast_multiply_fusion
  131.9 0.0 copy-done.1
  131.9 1.6 %copy.15 = f32[24,64,256]{2,1,0:T(8,128)} copy(f32[24,64,256]{2,0,1:T(8,128)S(1)} %broadcast_multiply_fusion) | data formatting | bytes 3145728
  (8 shorter events, 0.1 us)
Async XLA Ops:
  7.2 52.3 %all-gather.2.cloned.1.call-start = ((), (), s32[]{:S(2)}) async-start(), calls=%async_computation.1 | async-start | bytes 4718592 | tf_op jit(solution)/shard_map/all_gather | solution.py:46
  11.6 47.8 %copy-start = (f32[24,64,256]{2,0,1:T(8,128)S(1)}, f32[24,64,256]{2,0,1:T(8,128)}, u32[]{:S(2)}) copy-start(f32[24,64,256]{2,0,1:T(8,128)} %copy_multiply_fusion) | copy-start | bytes 4718596
  11.6 115.2 %reduce-scatter.2.cloned.1.call-start = ((), (), s32[]{:S(2)}) async-start(), calls=%async_computation.2 | async-start | bytes 98304 | tf_op jit(solution)/shard_map/reduce_scatter | solution.py:58
  114.3 17.6 %copy-start.1 = (f32[48]{0:T(128)}, f32[48]{0:T(128)S(1)}, u32[]{:S(2)}) copy-start(f32[48]{0:T(128)S(1)} %fusion.1) | copy-start | bytes 580
Sparse Core Ops, SparseCore 0:
  11.8 47.6 all-gather.1
  116.1 10.7 reduce-scatter.1
where the time goes:
time: 141 us; the launch traced here: 140 us
  waiting for transfers between devices  58.7 us (42%)
  blocking collectives  44.3 us (31%)
  other arithmetic  14.1 us (10%)
  between operations  14.1 us (10%)
  matrix products  5.76 us (4%)
  local copies, waits for them, and re-layouts  3.38 us (2%)
    all_gather x1, waiting for transfers between devices, shards(): portion = lax.all_gather(masked, 'grp', axis=0, tiled=True)  47.7 us
    psum x1, blocking collectives, shards(): gram_matrix = lax.psum(placed, ('grp', 'dom'))  39.5 us
    reduce_scatter x1, waiting for transfers between devices, shards(): lax.psum_scatter(partial_sum, 'grp', scatter_dimension=0, tiled=True)  10.9 us
    another operation x3, other arithmetic, solve_weights(): factor = jnp.linalg.cholesky(system)  5.06 us
    all_gather x1, blocking collectives, shards(): combined = lax.all_gather(own_share, 'grp', axis=0, tiled=True)  4.78 us
    dot_general x1, matrix products, inner_rows(): lax.dot_general(left_rows, right_rows, (((1,), (1,)), ((), ())), precisio...  4.46 us
    another operation x2, other arithmetic, solve_weights(): lax.linalg.triangular_solve(factor, halfway, left_side=True, lower=True,...  4.32 us
    mul x1, other arithmetic, shards(): masked = surplus * owners[:, :, None]  3.5 us
  transfers between devices with their start and end apart: 2, of which 2 were waited for; matrix products, arithmetic and copies ran while one was open for 0% of the time, Pallas kernels for 0%

commit v1 on v0

--- a/solution.py
+++ b/solution.py
@@ -49,7 +49,7 @@
     placed = lax.dynamic_update_slice(
         jnp.zeros((grid_total, grid_total), jnp.float32), products, (row_start, jnp.int32(0))
     )
-    gram_matrix = lax.psum(placed, ("grp", "dom"))
+    gram_matrix = lax.psum(lax.psum(placed, "dom"), "grp")
     coefficients = solve_weights(gram_matrix)
     own_weights = lax.dynamic_slice_in_dim(
         coefficients, lax.axis_index("grp") * local_count, local_count

time: 141 us -> 166 us (1.18)
  blocking collectives: 44.3 us -> 73.1 us
  waiting for transfers between devices: 58.7 us -> 55.2 us
    psum x1 -> x2, blocking collectives: 39.5 us -> 68.4 us  [shards(): gram_matrix = lax.psum(lax.psum(placed, 'dom'), 'grp')]
    reduce_scatter x1, waiting for transfers between devices: 10.9 us -> 7.41 us  [shards(): lax.psum_scatter(partial_sum, 'grp', scatter_dimension=0, tiled=True)]
where the time goes in v1:
time: 166 us
  blocking collectives  73.1 us (44%)
  waiting for transfers between devices  55.2 us (33%)
  other arithmetic  14.2 us (9%)
  between operations  14.1 us (8%)
  matrix products  5.75 us (3%)
  local copies, waits for them, and re-layouts  3.38 us (2%)
    psum x2, blocking collectives, shards(): gram_matrix = lax.psum(lax.psum(placed, 'dom'), 'grp')  68.4 us
    all_gather x1, waiting for transfers between devices, shards(): portion = lax.all_gather(masked, 'grp', axis=0, tiled=True)  47.7 us
    reduce_scatter x1, waiting for transfers between devices, shards(): lax.psum_scatter(partial_sum, 'grp', scatter_dimension=0, tiled=True)  7.41 us
    another operation x3, other arithmetic, solve_weights(): factor = jnp.linalg.cholesky(system)  5.06 us
    all_gather x1, blocking collectives, shards(): combined = lax.all_gather(own_share, 'grp', axis=0, tiled=True)  4.78 us
    dot_general x1, matrix products, inner_rows(): lax.dot_general(left_rows, right_rows, (((1,), (1,)), ((), ())), precisio...  4.46 us
    another operation x2, other arithmetic, solve_weights(): lax.linalg.triangular_solve(factor, halfway, left_side=True, lower=True,...  4.34 us
    mul x1, other arithmetic, shards(): masked = surplus * owners[:, :, None]  3.5 us
  transfers between devices with their start and end apart: 2, of which 2 were waited for; matrix products, arithmetic and copies ran while one was open for 0% of the time, Pallas kernels for 0%

profile of v1, /device:TPU:0, one launch (start us, length us, event | category | flops | bytes accessed | tf_op | source)
XLA Modules:
  0.0 165.8 jit_solution(12551827892473646628)
XLA Ops:
  7.2 0.0 all-gather.2.cloned.1.call-start
  7.3 0.8 compare_reduce_fusion
  8.0 0.1 copy.12
  8.1 3.5 %copy_multiply_fusion = f32[24,64,256]{2,0,1:T(8,128)} fusion(f32[24,64,256]{2,1,0:T(8,128)} %param.2, f32[24,64]{0,1:T(8,128)S(1)} %copy.12), kind=kLoop, calls=%fused_computation.1 | loop fusion | flops 393216 | bytes 3151872 | tf_op jit(solution)/shard_map/mul | solution.py:44
  11.6 0.0 copy-start
  11.6 0.0 all-gather.2.cloned.1.call-update
  11.6 0.0 reduce-scatter.2.cloned.1.call-start
  11.7 47.7 %all-gather.2.cloned.1.call-done = f32[48,64,256]{2,0,1:T(8,128)} async-done(((f32[24,64,256]{2,0,1:T(8,128)}), f32[48,64,256]{2,0,1:T(8,128)}) %all-gather.2.cloned.1.call-update) | async-done | bytes 3145744 | tf_op jit(solution)/shard_map/all_gather | solution.py:46
  59.4 0.0 copy-done
  59.4 4.5 %fusion = f32[48,48]{1,0:T(8,128)S(1)} fusion(f32[48,48]{1,0:T(8,128)S(1)} %broadcast_in_dim.5, s32[]{:T(128)S(6)} %select_n.63, f32[24,64,256]{2,0,1:T(8,128)S(1)} %copy-done, f32[48,64,256]{2,0,1:T(8,128)} %all-gather.2.cloned.1.call-done), kind=kOutput, calls=%fused_computation.3 | convolution fusion | flops 226492416 | bytes 4730884 | tf_op jit(solution)/shard_map/dot_general | solution.py:30
  63.9 61.0 %psum.14 = f32[48,48]{1,0:T(8,128)S(1)} all-reduce(f32[48,48]{1,0:T(8,128)S(1)} %fusion), channel_id=1, replica_groups=mesh['grp'=2,'dom'=16] {'dom'}, use_global_device_ids=true, to_apply=%region_1.2 | all-reduce | flops 2304 | bytes 18432 | tf_op jit(solution)/shard_map/psum | solution.py:52
  124.9 7.3 %psum.15 = f32[48,48]{1,0:T(8,128)S(1)} all-reduce(f32[48,48]{1,0:T(8,128)S(1)} %psum.14), channel_id=1, replica_groups=mesh['grp'=2,'dom'=16] {'grp'}, use_global_device_ids=true, to_apply=%region_2.3 | all-reduce | flops 2304 | bytes 18432 | tf_op jit(solution)/shard_map/psum | solution.py:52
  132.3 1.0 gather_fusion
  133.2 0.1 select_add_fusion
  133.3 0.1 copy.14
  133.4 0.1 fusion.5
  133.5 4.4 %cholesky.16 = f32[48,48]{1,0:T(8,128)S(1)} custom-call(f32[48,48]{1,0:T(8,128)S(1)} %fusion.5), custom_call_target="Cholesky" | custom-call | tf_op jit(solution)/shard_map/jit(cholesky)/cholesky | solution.py:20
  137.9 0.6 compare_reduce_fusion.1
  138.5 0.7 fusion.2
  139.2 3.7 %custom-call.8 = f32[1,48,48]{1,2,0:T(8,128)S(1)} custom-call(f32[1,48,48]{2,1,0:T(8,128)S(1)} %fusion.2), custom_call_target="InvertDiagBlocksLowerTriangular" | custom-call | tf_op jit(solution)/shard_map/triangular_solve | solution.py:23
  142.9 0.1 convolution_bitcast_fusion.2
  143.0 0.1 fusion.1
  143.2 0.0 copy-start.1
  143.2 1.0 fusion.7
  144.2 0.6 copy.19
  144.8 0.0 reduce-scatter.2.cloned.1.call-update
  144.8 7.4 %reduce-scatter.2.cloned.1.call-done = f32[32,256]{1,0:T(8,128)} async-done(((f32[64,256]{1,0:T(8,128)}), f32[32,256]{1,0:T(8,128)}) %reduce-scatter.2.cloned.1.call-update) | async-done | bytes 32784 | tf_op jit(solution)/shard_map/reduce_scatter | solution.py:58
  152.2 4.8 %all_gather.7 = f32[64,256]{1,0:T(8,128)S(1)} all-gather(f32[32,256]{1,0:T(8,128)} %reduce-scatter.2.cloned.1.call-done), channel_id=1, replica_groups=mesh['grp'=2,'dom'=16] {'grp'}, dimensions={0}, use_global_device_ids=true | all-gather | bytes 98304 | tf_op jit(solution)/shard_map/all_gather | solution.py:59
  157.0 0.3 broadcast_multiply_fusion
  157.3 0.0 copy-done.1
  157.3 1.6 copy.15
  (8 shorter events, 0.1 us)
Async XLA Ops:
  7.2 52.3 %all-gather.2.cloned.1.call-start = ((), (), s32[]{:S(2)}) async-start(), calls=%async_computation.1 | async-start | bytes 4718592 | tf_op jit(solution)/shard_map/all_gather | solution.py:46
  11.6 47.8 %copy-start = (f32[24,64,256]{2,0,1:T(8,128)S(1)}, f32[24,64,256]{2,0,1:T(8,128)}, u32[]{:S(2)}) copy-start(f32[24,64,256]{2,0,1:T(8,128)} %copy_multiply_fusion) | copy-start | bytes 4718596
  11.6 140.6 %reduce-scatter.2.cloned.1.call-start = ((), (), s32[]{:S(2)}) async-start(), calls=%async_computation.2 | async-start | bytes 98304 | tf_op jit(solution)/shard_map/reduce_scatter | solution.py:58
  143.2 14.1 %copy-start.1 = (f32[48]{0:T(128)}, f32[48]{0:T(128)S(1)}, u32[]{:S(2)}) copy-start(f32[48]{0:T(128)S(1)} %fusion.1) | copy-start | bytes 580
Sparse Core Ops, SparseCore 0:
  11.8 47.6 all-gather.1
  144.9 7.2 reduce-scatter.1
